TPU v7x, 32 devices: a whole 2x2x4 slice. The times are simulated.
32 devices in a mesh: blk: 16 (over z, y, x), row: 2 (over core).
Axes of the slice: x: 2, y: 2, z: 4, core: 2. Of those that a mesh axis runs over, the one named last changes fastest.
Arguments:
- genotypes: bfloat16 [128, 16, 2048], P('blk', None, 'row'), may hold values from 0 to 2
- assignment: int32 [16], replicated, may hold values from 0 to 15, each once
- snp_counts: int32 [16], replicated, may hold values from 1024 to 2048, as said below
- basis: float32 [16, 64, 2048], P('blk', None, 'row'), may hold values from -6 to 6
Outputs:
- image: float32 [16, 64, 2048], P('blk', None, 'row')
- new_basis: float32 [16, 64, 2048], P('blk', None, 'row')
- factor: float32 [16, 64, 64], P('blk')
Inputs may be any that keep to these rules, and one draw needn't show every extreme that they name: `assignment`: each block number appears exactly once. `snp_counts`: A block's SNPs fill its leading slots.
All inputs are finite; a program needn't handle non-finite values.
Results may differ from a plain program's by a relative error of at most 0.0021.
Values may be sent and summed in bfloat16 or wider, within the bound.
No kernel may reach another device: no remote copies, remote signals or barrier semaphores. Data moves between devices by JAX's collectives and lax.ppermute only.
A program may use at most 64 MiB of HBM per device.

v0:
```python
import jax
import jax.numpy as jnp
from jax import lax
from jax.sharding import PartitionSpec as P

epsilon = 1e-05
shrink_weight = 0.5


def body(genotypes, assignment, snp_counts, basis):
    ordered = jnp.take(genotypes, assignment, axis=1)
    regrouped = lax.all_to_all(ordered, "blk", split_axis=1, concat_axis=0, tiled=True)
    samples = regrouped.shape[0]
    owned = regrouped.shape[1]
    half_width = regrouped.shape[2]
    block_ids = lax.dynamic_slice_in_dim(assignment, lax.axis_index("blk") * owned, owned)
    catalog = jnp.arange(snp_counts.shape[0], dtype=jnp.int32)
    live_count = jnp.sum(
        jnp.where(block_ids[:, None] == catalog[None, :], snp_counts[None, :], 0), axis=1
    )
    columns = lax.axis_index("row") * half_width + jnp.arange(half_width, dtype=jnp.int32)
    live_mask = columns[None, :] < live_count[:, None]
    values = regrouped.astype(jnp.float32)
    col_mean = jnp.mean(values, axis=0)
    centered = values - col_mean[None]
    col_var = jnp.mean(centered * centered, axis=0)
    standard = jnp.where(
        live_mask[None], centered * lax.rsqrt(col_var + epsilon)[None], 0.0
    ).astype(jnp.bfloat16)
    inverse = 1.0 / samples
    partial_proj = jnp.einsum(
        "nbi,bri->brn",
        standard,
        basis,
        precision=lax.Precision.HIGHEST,
        preferred_element_type=jnp.float32,
    )
    projected = lax.psum(partial_proj, "row")
    product = (
        jnp.einsum(
            "nbi,brn->bri",
            standard,
            projected,
            precision=lax.Precision.HIGHEST,
            preferred_element_type=jnp.float32,
        )
        * inverse
    )
    image = shrink_weight * product + (1.0 - shrink_weight) * jnp.where(
        live_mask[:, None, :], basis, 0.0
    )
    gram_part = jnp.einsum("bri,bsi->brs", image, image, precision=lax.Precision.HIGHEST)
    gram_sum = lax.psum(gram_part, "row")
    factor = jnp.linalg.cholesky(gram_sum)
    new_basis = jax.scipy.linalg.solve_triangular(factor, image, lower=True)
    return (image, new_basis, factor)


def solution(mesh):
    in_specs = (P("blk", None, "row"), P(), P(), P("blk", None, "row"))
    out_specs = (P("blk", None, "row"), P("blk", None, "row"), P("blk", None, None))
    return jax.shard_map(body, mesh=mesh, in_specs=in_specs, out_specs=out_specs, check_vma=False)
```

profile of v0, /device:TPU:0, one launch (start us, length us, event | category | flops | bytes accessed | tf_op | source)
XLA Modules:
  0.0 44.3 jit_solution(11214147400684434349)
XLA Ops:
  0.6 0.0 copy-start
  0.6 0.0 copy-start.3
  0.7 0.7 %compare_and_fusion = pred[16]{0:T(512)(128)(4,1)S(1)} fusion(s32[16]{0:T(128)} %param.5), kind=kLoop, calls=%fused_computation.36 | loop fusion | flops 96 | bytes 80 | tf_op jit(solution)/shard_map/jit(_take)/and | solution.py:11
  1.4 0.0 copy-done.3
  1.4 0.2 copy-done
  1.6 1.3 %gather_fusion = bf16[16,8,1024]{2,0,1:T(8,128)(2,1)S(1)} fusion(bf16[8,16,1024]{2,1,0:T(8,128)(2,1)S(1)} %copy-done, s32[1024]{0:T(1024)S(1)} %pad_clamp_fusion), kind=kCustom, calls=%fused_computation | custom fusion | bytes 524352 | tf_op jit(solution)/shard_map/jit(_take)/gather | solution.py:11
  2.9 0.1 select_bitcast_fusion
  3.0 0.9 %copy.13 = bf16[8,16,1024]{2,0,1:T(8,128)(2,1)} copy(bf16[8,16,1024]{2,1,0:T(8,128)(2,1)S(1)} %select_bitcast_fusion) | data formatting | bytes 524288 | tf_op jit(solution)/shard_map/jit(_take)/select_n | solution.py:11
  3.9 8.3 %all-to-all-start = ((bf16[8,16,1024]{2,0,1:T(8,128)(2,1)}), bf16[8,16,1024]{2,0,1:T(8,128)(2,1)S(1)}, u32[]{:S(2)}, u32[]{:S(2)}) async-start(bf16[8,16,1024]{2,0,1:T(8,128)(2,1)} %copy.13), calls=%async_computation | async-start | bytes 524288 | tf_op jit(solution)/shard_map/all_to_all | solution.py:12
  12.2 0.6 %dynamic_slice.3 = s32[1]{0:T(128)} dynamic-slice(s32[16]{0:T(128)S(1)} %copy-done.3, s32[]{:T(128)S(6)} %select_n.50), dynamic_slice_sizes={1} | dynamic-slice | bytes 12 | tf_op jit(solution)/shard_map/dynamic_slice | solution.py:16
  12.8 0.0 copy-start.4
  12.8 0.7 %copy-done.4 = s32[16]{0:T(128)S(1)} copy-done((s32[16]{0:T(128)S(1)}, s32[16]{0:T(128)}, u32[]{:S(2)}) %copy-start.4) | copy-done | bytes 88
  13.5 1.3 %fusion.18 = s32[]{:T(128)} fusion(s32[16]{0:T(128)S(1)} %copy-done.4, s32[]{:T(128)} %bitcast), kind=kLoop, calls=%fused_computation.38 | loop fusion | flops 47 | bytes 72 | tf_op jit(solution)/shard_map/reduce_sum | solution.py:18
  14.8 0.7 %add_compare_fusion = pred[1024]{0:T(1024)(128)(4,1)S(1)} fusion(s32[]{:T(128)} %fusion.18, s32[]{:T(128)S(6)} %mul.56), kind=kLoop, calls=%fused_computation.32 | loop fusion | flops 2048 | bytes 1032 | tf_op jit(solution)/shard_map/lt | solution.py:22
  15.4 0.0 copy-start.2
  15.4 6.7 %all-to-all-done = bf16[8,16,1024]{2,0,1:T(8,128)(2,1)S(1)} async-done(((bf16[8,16,1024]{2,0,1:T(8,128)(2,1)}), bf16[8,16,1024]{2,0,1:T(8,128)(2,1)S(1)}, u32[]{:S(2)}, u32[]{:S(2)}) %all-to-all-start) | async-done | bytes 262176 | tf_op jit(solution)/shard_map/all_to_all | solution.py:12
  22.1 0.1 convert_reduce_fusion
  22.2 0.1 fusion.4
  22.3 0.0 copy-done.2
  22.3 0.4 convolution_bitcast_fusion.2
  22.7 3.4 %psum.14 = f32[64,128]{1,0:T(8,128)S(1)} all-reduce(f32[64,128]{1,0:T(8,128)S(1)} %convolution_bitcast_fusion.2), channel_id=1, replica_groups=mesh['blk'=16,'row'=2] {'row'}, use_global_device_ids=true, to_apply=%region_3.4 | all-reduce | flops 8192 | bytes 65536 | tf_op jit(solution)/shard_map/psum | solution.py:38
  26.1 0.3 fusion.1
  26.4 0.0 copy-start.1
  26.4 0.4 convolution_bitcast_fusion.1
  26.8 3.6 %psum.15 = f32[1,64,64]{1,2,0:T(8,128)S(1)} all-reduce(f32[1,64,64]{1,2,0:T(8,128)S(1)} %convolution_bitcast_fusion.1), channel_id=1, replica_groups=mesh['blk'=16,'row'=2] {'row'}, use_global_device_ids=true, to_apply=%region_4.5 | all-reduce | flops 4096 | bytes 32768 | tf_op jit(solution)/shard_map/psum | solution.py:53
  30.3 0.1 copy.15
  30.4 5.8 %custom-call.8 = f32[1,64,64]{2,1,0:T(8,128)S(1)} custom-call(f32[1,64,64]{2,1,0:T(8,128)S(1)} %fusion.16), custom_call_target="Cholesky" | custom-call | tf_op jit(solution)/shard_map/jit(cholesky)/cholesky | solution.py:54
  36.3 0.6 %compare_reduce_fusion = pred[]{:T(512)} fusion(f32[64]{0:T(128)S(1)} %select_reduce_fusion), kind=kLoop, calls=%fused_computation.35 | loop fusion | flops 127 | bytes 257 | tf_op jit(solution)/shard_map/jit(cholesky)/cholesky | solution.py:54
  37.0 1.3 %fusion.17 = (f32[1,64,64]{2,1,0:T(8,128)S(1)}, f32[1,64,64]{2,1,0:T(8,128)}) fusion(f32[1,64,64]{2,1,0:T(8,128)S(1)} %custom-call.8, pred[]{:T(512)} %compare_reduce_fusion), kind=kLoop, calls=%fused_computation.29 | loop fusion | flops 16384 | bytes 49153 | tf_op jit(solution)/shard_map/jit(_solve_triangular)/triangular_solve | solution.py:55
  38.2 4.9 %custom-call.9 = f32[1,64,64]{1,2,0:T(8,128)S(1)} custom-call(f32[1,64,64]{2,1,0:T(8,128)S(1)} %get-tuple-element.3), custom_call_target="InvertDiagBlocksLowerTriangular" | custom-call | tf_op jit(solution)/shard_map/jit(_solve_triangular)/triangular_solve | solution.py:55
  43.1 0.0 copy-done.1
  43.1 1.1 %convolution_bitcast_fusion = f32[1,64,1024]{2,1,0:T(8,128)} fusion(f32[1,64,1024]{2,1,0:T(8,128)S(1)} %fusion.1, f32[1,64,64]{1,2,0:T(8,128)S(1)} %custom-call.9), kind=kOutput, calls=%fused_computation.3 | convolution fusion | flops 50331648 | bytes 540672 | tf_op jit(solution)/shard_map/jit(_solve_triangular)/triangular_solve | solution.py:55
  (6 shorter events, 0.1 us)
Async XLA Ops:
  0.6 1.0 %copy-start = (bf16[8,16,1024]{2,1,0:T(8,128)(2,1)S(1)}, bf16[8,16,1024]{2,1,0:T(8,128)(2,1)}, u32[]{:S(2)}) copy-start(bf16[8,16,1024]{2,1,0:T(8,128)(2,1)} %param.4) | copy-start | bytes 786436
  0.6 0.7 %copy-start.3 = (s32[16]{0:T(128)S(1)}, s32[16]{0:T(128)}, u32[]{:S(2)}) copy-start(s32[16]{0:T(128)} %param.5) | copy-start | bytes 196
  3.9 18.2 %all-to-all-start = ((bf16[8,16,1024]{2,0,1:T(8,128)(2,1)}), bf16[8,16,1024]{2,0,1:T(8,128)(2,1)S(1)}, u32[]{:S(2)}, u32[]{:S(2)}) async-start(bf16[8,16,1024]{2,0,1:T(8,128)(2,1)} %copy.13), calls=%async_computation | async-start | bytes 524288 | tf_op jit(solution)/shard_map/all_to_all | solution.py:12
  12.8 0.7 %copy-start.4 = (s32[16]{0:T(128)S(1)}, s32[16]{0:T(128)}, u32[]{:S(2)}) copy-start(s32[16]{0:T(128)} %param.6) | copy-start | bytes 196
  15.4 6.9 %copy-start.2 = (f32[1,64,1024]{2,1,0:T(8,128)S(1)}, f32[1,64,1024]{2,1,0:T(8,128)}, u32[]{:S(2)}) copy-start(f32[1,64,1024]{2,1,0:T(8,128)} %param.7) | copy-start | bytes 786436
  26.4 16.8 %copy-start.1 = (f32[1,64,1024]{2,1,0:T(8,128)}, f32[1,64,1024]{2,1,0:T(8,128)S(1)}, u32[]{:S(2)}) copy-start(f32[1,64,1024]{2,1,0:T(8,128)S(1)} %fusion.1) | copy-start | bytes 786436
where the time goes:
time: 44.6 us; the launch traced here: 44.3 us
  other arithmetic  15.6 us (35%)
  starting transfers between devices  8.34 us (19%)
  blocking collectives  6.97 us (16%)
  waiting for transfers between devices  6.68 us (15%)
  local copies, waits for them, and re-layouts  3.73 us (8%)
  matrix products  2.15 us (5%)
  between operations  0.79 us (2%)
    all_to_all x1, starting transfers between devices, body(): lax.all_to_all(ordered, 'blk', split_axis=1, concat_axis=0, tiled=True)  8.34 us
    all_to_all x1, waiting for transfers between devices, body(): lax.all_to_all(ordered, 'blk', split_axis=1, concat_axis=0, tiled=True)  6.68 us
    another operation x3, other arithmetic, body(): factor = jnp.linalg.cholesky(gram_sum)  6.52 us
    another operation x2, other arithmetic, body(): new_basis = jax.scipy.linalg.solve_triangular(factor, image, lower=True)  6.16 us
    psum x1, blocking collectives, body(): gram_sum = lax.psum(gram_part, 'row')  3.57 us
    psum x1, blocking collectives, body(): projected = lax.psum(partial_proj, 'row')  3.41 us
    gather x1, local copies, waits for them, and re-layouts, body(): ordered = jnp.take(genotypes, assignment, axis=1)  1.31 us
    reduce_sum x1, other arithmetic, body(): jnp.sum(jnp.where(block_ids[:, None] == catalog[None, :], snp_counts[None...  1.27 us
  transfers between devices with their start and end apart: 1, of which 1 were waited for; matrix products, arithmetic and copies ran while one was open for 6% of the time, Pallas kernels for 0%

commit v1 on v0

--- a/solution.py
+++ b/solution.py
@@ -9,7 +9,11 @@
 
 def body(genotypes, assignment, snp_counts, basis):
     ordered = jnp.take(genotypes, assignment, axis=1)
-    regrouped = lax.all_to_all(ordered, "blk", split_axis=1, concat_axis=0, tiled=True)
+    plain = lax.axis_size("blk")
+    passed = jnp.split(ordered, plain, axis=1)
+    r2 = jnp.stack(passed)
+    side_arr = lax.all_to_all(r2, "blk", 0, 0)
+    regrouped = jnp.concatenate(side_arr, axis=0)
     samples = regrouped.shape[0]
     owned = regrouped.shape[1]
     half_width = regrouped.shape[2]

time: 44.6 us -> 54.1 us (1.21)
  local copies, waits for them, and re-layouts: 3.73 us -> 13.2 us
    unnamed x10 -> x25, local copies, waits for them, and re-layouts: 0.9 us -> 10.1 us
    select_n x1 -> x0, local copies, waits for them, and re-layouts: 0.85 us -> none  [body(): ordered = jnp.take(genotypes, assignment, axis=1)]
    select_n x2, other arithmetic: 0.1 us -> 0.82 us  [body(): ordered = jnp.take(genotypes, assignment, axis=1)]
    and x1, other arithmetic: 0.73 us -> 0.01 us  [body(): ordered = jnp.take(genotypes, assignment, axis=1)]
    another operation x0 -> x1, local copies, waits for them, and re-layouts: none -> 0.61 us  [body(): r2 = jnp.stack(passed)]
    split x0 -> x1, local copies, waits for them, and re-layouts: none -> 0.56 us  [body(): passed = jnp.split(ordered, plain, axis=1)]
  transfers between devices with their start and end apart: 1 -> 1, of which waited for: 1 -> 1; matrix products, arithmetic and copies ran while one was open for 6% -> 5% of each run, Pallas kernels for 0% -> 0%
where the time goes in v1:
time: 54.1 us; the launch traced here: 53.8 us
  other arithmetic  15.6 us (29%)
  local copies, waits for them, and re-layouts  13.2 us (24%)
  starting transfers between devices  8.34 us (15%)
  blocking collectives  6.97 us (13%)
  waiting for transfers between devices  6.68 us (12%)
  matrix products  2.15 us (4%)
  between operations  0.81 us (1%)
    unnamed x25, local copies, waits for them, and re-layouts  10.1 us
    all_to_all x1, starting transfers between devices, body(): side_arr = lax.all_to_all(r2, 'blk', 0, 0)  8.34 us
    all_to_all x1, waiting for transfers between devices, body(): side_arr = lax.all_to_all(r2, 'blk', 0, 0)  6.68 us
    another operation x3, other arithmetic, body(): factor = jnp.linalg.cholesky(gram_sum)  6.52 us
    another operation x2, other arithmetic, body(): new_basis = jax.scipy.linalg.solve_triangular(factor, image, lower=True)  6.16 us
    psum x1, blocking collectives, body(): gram_sum = lax.psum(gram_part, 'row')  3.57 us
    psum x1, blocking collectives, body(): projected = lax.psum(partial_proj, 'row')  3.41 us
    gather x1, local copies, waits for them, and re-layouts, body(): ordered = jnp.take(genotypes, assignment, axis=1)  1.31 us
  transfers between devices with their start and end apart: 1, of which 1 were waited for; matrix products, arithmetic and copies ran while one was open for 5% of the time, Pallas kernels for 0%

profile of v1, /device:TPU:0, one launch (start us, length us, event | category | flops | bytes accessed | tf_op | source)
XLA Modules:
  0.0 53.8 jit_solution(6985674774231968089)
XLA Ops:
  0.6 0.0 copy-start
  0.6 0.0 copy-start.3
  0.7 0.7 %compare_select_fusion = s32[16]{0:T(128)S(1)} fusion(s32[16]{0:T(128)} %param.5), kind=kLoop, calls=%fused_computation.49 | loop fusion | flops 48 | bytes 128 | tf_op jit(solution)/shard_map/jit(_take)/jit(_where)/select_n | solution.py:11
  1.4 0.0 copy-done.3
  1.4 0.2 copy-done
  1.6 1.3 %gather_fusion = bf16[16,8,1024]{2,0,1:T(8,128)(2,1)S(1)} fusion(bf16[8,16,1024]{2,1,0:T(8,128)(2,1)S(1)} %copy-done, s32[1024]{0:T(1024)S(1)} %pad_clamp_fusion), kind=kCustom, calls=%fused_computation | custom fusion | bytes 524352 | tf_op jit(solution)/shard_map/jit(_take)/gather | solution.py:11
  2.9 0.1 select_bitcast_fusion
  3.0 0.6 %fusion.21 = (bf16[8,1,1024]{2,1,0:T(2,128)(2,1)S(1)}, bf16[8,1,1024]{2,1,0:T(2,128)(2,1)S(1)}, bf16[8,1,1024]{2,1,0:T(2,128)(2,1)S(1)}, bf16[8,1,1024]{2,1,0:T(...) fusion(bf16[8,16,1024]{2,1,0:T(8,128)(2,1)S(1)} %select_bitcast, ...), kind=kLoop, calls=%fused_computation.57 | loop fusion | bytes 524288 | tf_op jit(solution)/shard_map/split | solution.py:13
  3.6 0.6 %constant_dynamic-update-slice_fusion.15 = bf16[16,8,1,1024]{3,1,2,0:T(8,128)(2,1)} fusion(bf16[8,1,1024]{2,1,0:T(2,128)(2,1)S(1)} %get-tuple-element.20), kind=kLoop, calls=%fused_computation.37 | loop fusion | bytes 32768
  4.2 0.6 %constant_dynamic-update-slice_fusion.14 = bf16[16,8,1,1024]{3,1,2,0:T(8,128)(2,1)} fusion(bf16[16,8,1,1024]{3,1,2,0:T(8,128)(2,1)} %constant_dynamic-update-slice_fusion.15, bf16[8,1,1024]{2,1,0:T(2,128)(2,1)S(1)} %get-tuple-element.19), kind=kLoop, calls=%fused_computation.36 | loop fusion | bytes 32768
  4.8 0.6 %constant_dynamic-update-slice_fusion.13 = bf16[16,8,1,1024]{3,1,2,0:T(8,128)(2,1)} fusion(bf16[16,8,1,1024]{3,1,2,0:T(8,128)(2,1)} %constant_dynamic-update-slice_fusion.14, bf16[8,1,1024]{2,1,0:T(2,128)(2,1)S(1)} %get-tuple-element.18), kind=kLoop, calls=%fused_computation.35 | loop fusion | bytes 32768
  5.4 0.6 %constant_dynamic-update-slice_fusion.12 = bf16[16,8,1,1024]{3,1,2,0:T(8,128)(2,1)} fusion(bf16[16,8,1,1024]{3,1,2,0:T(8,128)(2,1)} %constant_dynamic-update-slice_fusion.13, bf16[8,1,1024]{2,1,0:T(2,128)(2,1)S(1)} %get-tuple-element.17), kind=kLoop, calls=%fused_computation.34 | loop fusion | bytes 32768
  6.1 0.6 %constant_dynamic-update-slice_fusion.11 = bf16[16,8,1,1024]{3,1,2,0:T(8,128)(2,1)} fusion(bf16[16,8,1,1024]{3,1,2,0:T(8,128)(2,1)} %constant_dynamic-update-slice_fusion.12, bf16[8,1,1024]{2,1,0:T(2,128)(2,1)S(1)} %get-tuple-element.16), kind=kLoop, calls=%fused_computation.33 | loop fusion | bytes 32768
  6.7 0.6 %constant_dynamic-update-slice_fusion.10 = bf16[16,8,1,1024]{3,1,2,0:T(8,128)(2,1)} fusion(bf16[16,8,1,1024]{3,1,2,0:T(8,128)(2,1)} %constant_dynamic-update-slice_fusion.11, bf16[8,1,1024]{2,1,0:T(2,128)(2,1)S(1)} %get-tuple-element.15), kind=kLoop, calls=%fused_computation.32 | loop fusion | bytes 32768
  7.3 0.6 %constant_dynamic-update-slice_fusion.9 = bf16[16,8,1,1024]{3,1,2,0:T(8,128)(2,1)} fusion(bf16[16,8,1,1024]{3,1,2,0:T(8,128)(2,1)} %constant_dynamic-update-slice_fusion.10, bf16[8,1,1024]{2,1,0:T(2,128)(2,1)S(1)} %get-tuple-element.14), kind=kLoop, calls=%fused_computation.31 | loop fusion | bytes 32768
  7.9 0.6 %constant_dynamic-update-slice_fusion.8 = bf16[16,8,1,1024]{3,1,2,0:T(8,128)(2,1)} fusion(bf16[16,8,1,1024]{3,1,2,0:T(8,128)(2,1)} %constant_dynamic-update-slice_fusion.9, bf16[8,1,1024]{2,1,0:T(2,128)(2,1)S(1)} %get-tuple-element.13), kind=kLoop, calls=%fused_computation.30 | loop fusion | bytes 32768
  8.5 0.6 %constant_dynamic-update-slice_fusion.7 = bf16[16,8,1,1024]{3,1,2,0:T(8,128)(2,1)} fusion(bf16[16,8,1,1024]{3,1,2,0:T(8,128)(2,1)} %constant_dynamic-update-slice_fusion.8, bf16[8,1,1024]{2,1,0:T(2,128)(2,1)S(1)} %get-tuple-element.12), kind=kLoop, calls=%fused_computation.29 | loop fusion | bytes 32768
  9.1 0.6 %constant_dynamic-update-slice_fusion.6 = bf16[16,8,1,1024]{3,1,2,0:T(8,128)(2,1)} fusion(bf16[16,8,1,1024]{3,1,2,0:T(8,128)(2,1)} %constant_dynamic-update-slice_fusion.7, bf16[8,1,1024]{2,1,0:T(2,128)(2,1)S(1)} %get-tuple-element.11), kind=kLoop, calls=%fused_computation.28 | loop fusion | bytes 32768
  9.7 0.6 %constant_dynamic-update-slice_fusion.5 = bf16[16,8,1,1024]{3,1,2,0:T(8,128)(2,1)} fusion(bf16[16,8,1,1024]{3,1,2,0:T(8,128)(2,1)} %constant_dynamic-update-slice_fusion.6, bf16[8,1,1024]{2,1,0:T(2,128)(2,1)S(1)} %get-tuple-element.10), kind=kLoop, calls=%fused_computation.27 | loop fusion | bytes 32768
  10.3 0.6 %constant_dynamic-update-slice_fusion.4 = bf16[16,8,1,1024]{3,1,2,0:T(8,128)(2,1)} fusion(bf16[16,8,1,1024]{3,1,2,0:T(8,128)(2,1)} %constant_dynamic-update-slice_fusion.5, bf16[8,1,1024]{2,1,0:T(2,128)(2,1)S(1)} %get-tuple-element.9), kind=kLoop, calls=%fused_computation.26 | loop fusion | bytes 32768
  11.0 0.6 %constant_dynamic-update-slice_fusion.3 = bf16[16,8,1,1024]{3,1,2,0:T(8,128)(2,1)} fusion(bf16[16,8,1,1024]{3,1,2,0:T(8,128)(2,1)} %constant_dynamic-update-slice_fusion.4, bf16[8,1,1024]{2,1,0:T(2,128)(2,1)S(1)} %get-tuple-element.8), kind=kLoop, calls=%fused_computation.25 | loop fusion | bytes 32768
  11.6 0.6 %constant_dynamic-update-slice_fusion.2 = bf16[16,8,1,1024]{3,1,2,0:T(8,128)(2,1)} fusion(bf16[16,8,1,1024]{3,1,2,0:T(8,128)(2,1)} %constant_dynamic-update-slice_fusion.3, bf16[8,1,1024]{2,1,0:T(2,128)(2,1)S(1)} %get-tuple-element.7), kind=kLoop, calls=%fused_computation.24 | loop fusion | bytes 32768
  12.2 0.6 %constant_dynamic-update-slice_fusion.1 = bf16[16,8,1,1024]{3,1,2,0:T(8,128)(2,1)} fusion(bf16[16,8,1,1024]{3,1,2,0:T(8,128)(2,1)} %constant_dynamic-update-slice_fusion.2, bf16[8,1,1024]{2,1,0:T(2,128)(2,1)S(1)} %get-tuple-element.6), kind=kLoop, calls=%fused_computation.23 | loop fusion | bytes 32768
  12.8 0.6 %constant_dynamic-update-slice_fusion = bf16[16,8,1,1024]{3,1,2,0:T(8,128)(2,1)} fusion(bf16[16,8,1,1024]{3,1,2,0:T(8,128)(2,1)} %constant_dynamic-update-slice_fusion.1, bf16[8,1,1024]{2,1,0:T(2,128)(2,1)S(1)} %get-tuple-element.5), kind=kLoop, calls=%fused_computation.22 | loop fusion | bytes 32768 | tf_op jit(solution)/shard_map/stack | solution.py:14
  13.4 8.3 %all-to-all-start = ((bf16[16,8,1,1024]{3,1,2,0:T(8,128)(2,1)}), bf16[16,8,1,1024]{3,1,2,0:T(8,128)(2,1)S(1)}, u32[]{:S(2)}, u32[]{:S(2)}) async-start(bf16[16,8,1,1024]{3,1,2,0:T(8,128)(2,1)} %constant_dynamic-update-slice_fusion), calls=%async_computation | async-start | bytes 524288 | tf_op jit(solution)/shard_map/all_to_all | solution.py:15
  21.8 0.6 %dynamic_slice.3 = s32[1]{0:T(128)} dynamic-slice(s32[16]{0:T(128)S(1)} %copy-done.3, s32[]{:T(128)S(6)} %select_n.50), dynamic_slice_sizes={1} | dynamic-slice | bytes 12 | tf_op jit(solution)/shard_map/dynamic_slice | solution.py:20
  22.4 0.0 copy-start.4
  22.4 0.7 %copy-done.4 = s32[16]{0:T(128)S(1)} copy-done((s32[16]{0:T(128)S(1)}, s32[16]{0:T(128)}, u32[]{:S(2)}) %copy-start.4) | copy-done | bytes 88
  23.0 1.3 %fusion.18 = s32[]{:T(128)} fusion(s32[16]{0:T(128)S(1)} %copy-done.4, s32[]{:T(128)} %bitcast), kind=kLoop, calls=%fused_computation.54 | loop fusion | flops 47 | bytes 72 | tf_op jit(solution)/shard_map/reduce_sum | solution.py:22
  24.3 0.7 %add_compare_fusion = pred[1024]{0:T(1024)(128)(4,1)S(1)} fusion(s32[]{:T(128)} %fusion.18, s32[]{:T(128)S(6)} %mul.56), kind=kLoop, calls=%fused_computation.48 | loop fusion | flops 2048 | bytes 1032 | tf_op jit(solution)/shard_map/lt | solution.py:26
  24.9 0.0 copy-start.2
  25.0 6.7 %all-to-all-done = bf16[16,8,1,1024]{3,1,2,0:T(8,128)(2,1)S(1)} async-done(((bf16[16,8,1,1024]{3,1,2,0:T(8,128)(2,1)}), bf16[16,8,1,1024]{3,1,2,0:T(8,128)(2,1)S(1)}, u32[]{:S(2)}, u32[]{:S(2)}) %all-to-all-start) | async-done | bytes 262176 | tf_op jit(solution)/shard_map/all_to_all | solution.py:15
  31.6 0.1 convert_reduce_fusion
  31.7 0.1 fusion.8
  31.8 0.0 copy-done.2
  31.8 0.4 convolution_bitcast_fusion.2
  32.2 3.4 %psum.14 = f32[64,128]{1,0:T(8,128)S(1)} all-reduce(f32[64,128]{1,0:T(8,128)S(1)} %convolution_bitcast_fusion.2), channel_id=1, replica_groups=mesh['blk'=16,'row'=2] {'row'}, use_global_device_ids=true, to_apply=%region_3.4 | all-reduce | flops 8192 | bytes 65536 | tf_op jit(solution)/shard_map/psum | solution.py:42
  35.6 0.3 fusion.1
  35.9 0.0 copy-start.1
  35.9 0.4 convolution_bitcast_fusion.1
  36.3 3.6 %psum.15 = f32[1,64,64]{1,2,0:T(8,128)S(1)} all-reduce(f32[1,64,64]{1,2,0:T(8,128)S(1)} %convolution_bitcast_fusion.1), channel_id=1, replica_groups=mesh['blk'=16,'row'=2] {'row'}, use_global_device_ids=true, to_apply=%region_4.5 | all-reduce | flops 4096 | bytes 32768 | tf_op jit(solution)/shard_map/psum | solution.py:57
  39.9 0.1 copy.160
  40.0 5.8 %custom-call.8 = f32[1,64,64]{2,1,0:T(8,128)S(1)} custom-call(f32[1,64,64]{2,1,0:T(8,128)S(1)} %fusion.16), custom_call_target="Cholesky" | custom-call | tf_op jit(solution)/shard_map/jit(cholesky)/cholesky | solution.py:58
  45.8 0.6 %compare_reduce_fusion = pred[]{:T(512)} fusion(f32[64]{0:T(128)S(1)} %select_reduce_fusion), kind=kLoop, calls=%fused_computation.51 | loop fusion | flops 127 | bytes 257 | tf_op jit(solution)/shard_map/jit(cholesky)/cholesky | solution.py:58
  46.5 1.3 %fusion.17 = (f32[1,64,64]{2,1,0:T(8,128)S(1)}, f32[1,64,64]{2,1,0:T(8,128)}) fusion(f32[1,64,64]{2,1,0:T(8,128)S(1)} %custom-call.8, pred[]{:T(512)} %compare_reduce_fusion), kind=kLoop, calls=%fused_computation.45 | loop fusion | flops 16384 | bytes 49153 | tf_op jit(solution)/shard_map/jit(_solve_triangular)/triangular_solve | solution.py:59
  47.7 4.9 %custom-call.9 = f32[1,64,64]{1,2,0:T(8,128)S(1)} custom-call(f32[1,64,64]{2,1,0:T(8,128)S(1)} %get-tuple-element.3), custom_call_target="InvertDiagBlocksLowerTriangular" | custom-call | tf_op jit(solution)/shard_map/jit(_solve_triangular)/triangular_solve | solution.py:59
  52.6 0.0 copy-done.1
  52.7 1.1 %convolution_bitcast_fusion = f32[1,64,1024]{2,1,0:T(8,128)} fusion(f32[1,64,1024]{2,1,0:T(8,128)S(1)} %fusion.1, f32[1,64,64]{1,2,0:T(8,128)S(1)} %custom-call.9), kind=kOutput, calls=%fused_computation.3 | convolution fusion | flops 50331648 | bytes 540672 | tf_op jit(solution)/shard_map/jit(_solve_triangular)/triangular_solve | solution.py:59
  (6 shorter events, 0.1 us)
Async XLA Ops:
  0.6 1.0 %copy-start = (bf16[8,16,1024]{2,1,0:T(8,128)(2,1)S(1)}, bf16[8,16,1024]{2,1,0:T(8,128)(2,1)}, u32[]{:S(2)}) copy-start(bf16[8,16,1024]{2,1,0:T(8,128)(2,1)} %param.4) | copy-start | bytes 786436
  0.6 0.7 %copy-start.3 = (s32[16]{0:T(128)S(1)}, s32[16]{0:T(128)}, u32[]{:S(2)}) copy-start(s32[16]{0:T(128)} %param.5) | copy-start | bytes 196
  13.4 18.2 %all-to-all-start = ((bf16[16,8,1,1024]{3,1,2,0:T(8,128)(2,1)}), bf16[16,8,1,1024]{3,1,2,0:T(8,128)(2,1)S(1)}, u32[]{:S(2)}, u32[]{:S(2)}) async-start(bf16[16,8,1,1024]{3,1,2,0:T(8,128)(2,1)} %constant_dynamic-update-slice_fusion), calls=%async_computation | async-start | bytes 524288 | tf_op jit(solution)/shard_map/all_to_all | solution.py:15
  22.4 0.7 %copy-start.4 = (s32[16]{0:T(128)S(1)}, s32[16]{0:T(128)}, u32[]{:S(2)}) copy-start(s32[16]{0:T(128)} %param.6) | copy-start | bytes 196
  24.9 6.9 %copy-start.2 = (f32[1,64,1024]{2,1,0:T(8,128)S(1)}, f32[1,64,1024]{2,1,0:T(8,128)}, u32[]{:S(2)}) copy-start(f32[1,64,1024]{2,1,0:T(8,128)} %param.7) | copy-start | bytes 786436
  35.9 16.8 %copy-start.1 = (f32[1,64,1024]{2,1,0:T(8,128)}, f32[1,64,1024]{2,1,0:T(8,128)S(1)}, u32[]{:S(2)}) copy-start(f32[1,64,1024]{2,1,0:T(8,128)S(1)} %fusion.1) | copy-start | bytes 786436
